TPU v7x, 32 devices: a whole 2x2x4 slice. The times are simulated.
32 devices in a mesh: ulysses: 8 (over z, x), blk: 4 (over y, core).
Axes of the slice: x: 2, y: 2, z: 4, core: 2. Of those that a mesh axis runs over, the one named last changes fastest.
Arguments:
- queries: bfloat16 [4, 512, 4096], P('blk', 'ulysses'), may hold values from -6 to 6
- key_rows: bfloat16 [4, 512, 1024], P('blk', 'ulysses'), may hold values from -6 to 6
- value_rows: bfloat16 [4, 512, 1024], P('blk', 'ulysses'), may hold values from -6 to 6
- tile_segment: int32 [16], replicated, may hold values from 0 to 3, never falling along the last dimension, each value on 1 to 8 neighbouring positions
Outputs:
- attended: bfloat16 [4, 512, 4096], P('blk', 'ulysses')
Inputs may be any that keep to these rules, and one draw needn't show every extreme that they name: `tile_segment`: segment numbers never fall along the sequence and each segment covers 1 to 8 tiles.
All inputs are finite; a program needn't handle non-finite values.
Results may differ from a plain program's by a relative error of at most 0.0045.
Values may be sent and summed in bfloat16 or wider, within the bound.
A program may use at most 64 MiB of HBM per device.

v0:
```python
import math
import jax
import jax.numpy as jnp
from jax import lax
from jax.sharding import PartitionSpec as P

HEAD_DIM = 128
TILE = 128
masked_score = -1e30


def segment_of(positions, tile_segment):
    tiles_total = tile_segment.shape[0]
    matches = (positions // TILE)[:, None] == jnp.arange(tiles_total, dtype=jnp.int32)[None, :]
    return jnp.sum(jnp.where(matches, tile_segment[None, :], 0), axis=1)


def visible(query_pos, query_seg, key_pos, key_seg):
    earlier = key_pos[None, :] <= query_pos[:, None]
    same_image = (key_seg[None, :] == query_seg[:, None]) & (query_seg[:, None] % 2 == 1)
    return earlier | same_image


def widen(source_rows, groups):
    tokens_dev = source_rows.shape[1]
    heads_here = source_rows.shape[2] // HEAD_DIM
    factor = max(1, groups // heads_here)
    spread = jnp.repeat(source_rows.reshape(1, tokens_dev, heads_here, HEAD_DIM), factor, axis=2)
    return spread.reshape(1, tokens_dev, heads_here * factor * HEAD_DIM)


def same_rows(row_ids):
    return row_ids


def update(current, allowed, query_block, key_block, value_block):
    maxima, denominators, weighted = current
    scores = jnp.einsum(
        "qkgd,skd->kgqs", query_block, key_block, preferred_element_type=jnp.float32
    )
    scores = jnp.where(allowed[None, None], scores * HEAD_DIM ** (-0.5), masked_score)
    new_max = jnp.maximum(maxima, jnp.max(scores, axis=3))
    weights = jnp.where(allowed[None, None], jnp.exp(scores - new_max[..., None]), 0.0)
    factor = jnp.exp(maxima - new_max)
    denominators = factor * denominators + jnp.sum(weights, axis=3)
    product = jnp.einsum(
        "kgqs,skd->kgqd",
        weights.astype(jnp.bfloat16),
        value_block,
        preferred_element_type=jnp.float32,
    )
    weighted = factor[..., None] * weighted + product
    return (new_max, denominators, weighted)


def keep_state(current, allowed, query_block, key_block, value_block):
    return current


def build_fold(query_rows, query_pos, tile_segment, key_position, kv_width):
    rows_total = query_rows.shape[0]
    kv_local = kv_width // HEAD_DIM
    group_size = query_rows.shape[1] // HEAD_DIM // kv_local
    shaped = query_rows.reshape(rows_total, kv_local, group_size, HEAD_DIM)
    query_seg = segment_of(query_pos, tile_segment)
    half_rows = rows_total // 2

    def fold_step(running, portion, offset):
        key_part, value_part = portion
        portion_rows = key_part.shape[0]
        block_rows = math.gcd(portion_rows, 512)
        block_total = portion_rows // block_rows
        key_blocks = key_part.reshape(block_total, block_rows, kv_local, HEAD_DIM)
        value_blocks = value_part.reshape(block_total, block_rows, kv_local, HEAD_DIM)

        def one_block(halves, inputs):
            key_block, value_block, block_number = inputs
            key_pos = key_position(
                block_number * block_rows + jnp.arange(block_rows, dtype=jnp.int32)
            )
            key_seg = segment_of(key_pos, tile_segment)
            results = []
            for half_index in range(2):
                row_low = half_index * half_rows
                row_high = row_low + half_rows
                allowed = visible(
                    query_pos[row_low:row_high], query_seg[row_low:row_high], key_pos, key_seg
                )
                results.append(
                    lax.cond(
                        jnp.any(allowed),
                        update,
                        keep_state,
                        halves[half_index],
                        allowed,
                        shaped[row_low:row_high],
                        key_block,
                        value_block,
                    )
                )
            return ((results[0], results[1]), None)

        running, unused = lax.scan(
            one_block, running, (key_blocks, value_blocks, jnp.arange(block_total, dtype=jnp.int32))
        )
        return running

    def empty_half():
        return (
            jnp.full((kv_local, group_size, half_rows), masked_score, jnp.float32),
            jnp.zeros((kv_local, group_size, half_rows), jnp.float32),
            jnp.zeros((kv_local, group_size, half_rows, HEAD_DIM), jnp.float32),
        )

    return (fold_step, (empty_half(), empty_half()))


def finish(running):
    outputs = [weighted / denominators[..., None] for maxima, denominators, weighted in running]
    joined = jnp.concatenate(outputs, axis=2)
    kv_local, group_size, rows_total, head_dim = joined.shape
    joined = jnp.transpose(joined, (2, 0, 1, 3)).reshape(
        rows_total, kv_local * group_size * head_dim
    )
    return joined.astype(jnp.bfloat16)


def local(queries, key_rows, value_rows, tile_segment):
    ulysses_count = lax.axis_size("ulysses")
    tokens_dev = queries.shape[1]
    block_len = tokens_dev * ulysses_count
    block_index = lax.axis_index("blk")
    local_rows = jnp.arange(block_len, dtype=jnp.int32)
    moved = (
        lax.all_to_all(queries, "ulysses", split_axis=2, concat_axis=1, tiled=True),
        lax.all_to_all(
            widen(key_rows, ulysses_count), "ulysses", split_axis=2, concat_axis=1, tiled=True
        ),
        lax.all_to_all(
            widen(value_rows, ulysses_count), "ulysses", split_axis=2, concat_axis=1, tiled=True
        ),
    )
    query_rows, key_local, value_local = (moved[0][0], moved[1][0], moved[2][0])
    query_pos = block_index * block_len + local_rows
    fold_step, initial = build_fold(
        query_rows, query_pos, tile_segment, same_rows, key_local.shape[1]
    )
    running = fold_step(
        initial,
        (
            lax.all_gather(key_local, "blk", axis=0, tiled=True),
            lax.all_gather(value_local, "blk", axis=0, tiled=True),
        ),
        jnp.int32(0),
    )
    attended = lax.all_to_all(
        finish(running)[None], "ulysses", split_axis=1, concat_axis=2, tiled=True
    )
    return attended


def solution(mesh):
    return jax.shard_map(
        local,
        mesh=mesh,
        in_specs=(
            P("blk", "ulysses", None),
            P("blk", "ulysses", None),
            P("blk", "ulysses", None),
            P(),
        ),
        out_specs=P("blk", "ulysses", None),
        check_vma=False,
    )
```

profile of v0, /device:TPU:4, one launch (start us, length us, event | category | flops | bytes accessed | tf_op | source)
XLA Modules:
  0.0 138.4 jit_solution(7677934682182908862)
XLA Ops:
  0.0 1.3 copy.59
  1.3 0.6 broadcast.215
  1.9 2.3 %reduce.4 = bf16[1024,64]{1,0:T(8,128)(2,1)S(1)} reduce(bf16[1024,1,64]{2,1,0:T(2,128)(2,1)S(1)} %bitcast.162, bf16[]{:T(256)} %broadcast.215), dimensions={1}, to_apply=%bitcast.126.reduce_sub_computation | reduce | bytes 262146
  4.2 0.9 reshape.154
  5.1 5.8 %all-to-all-start = ((bf16[8,2,4096]{2,1,0:T(2,128)(2,1)}), bf16[8,2,4096]{2,1,0:T(2,128)(2,1)S(1)}, u32[]{:S(2)}, u32[]{:S(2)}) async-start(bf16[8,2,4096]{2,1,0:T(2,128)(2,1)} %reshape.154), calls=%async_computation | async-start | bytes 262144 | tf_op jit(solution)/shard_map/all_to_all | solution.py:136
  11.3 2.3 %reduce.5 = bf16[1024,64]{1,0:T(8,128)(2,1)S(1)} reduce(bf16[1024,1,64]{2,1,0:T(2,128)(2,1)S(1)} %bitcast.163, bf16[]{:T(256)} %broadcast.215), dimensions={1}, to_apply=%bitcast.128.reduce_sub_computation | reduce | bytes 262146
  13.6 0.9 reshape.156
  14.5 3.7 %all-to-all-done = bf16[8,2,4096]{2,1,0:T(2,128)(2,1)S(1)} async-done(((bf16[8,2,4096]{2,1,0:T(2,128)(2,1)}), bf16[8,2,4096]{2,1,0:T(2,128)(2,1)S(1)}, u32[]{:S(2)}, u32[]{:S(2)}) %all-to-all-start) | async-done | bytes 131104 | tf_op jit(solution)/shard_map/all_to_all | solution.py:136
  18.2 3.4 %all-to-all-start.1 = ((bf16[8,2,4096]{2,1,0:T(2,128)(2,1)}), bf16[8,2,4096]{2,1,0:T(2,128)(2,1)S(1)}, u32[]{:S(2)}, u32[]{:S(2)}) async-start(bf16[8,2,4096]{2,1,0:T(2,128)(2,1)} %reshape.156), calls=%async_computation.1 | async-start | bytes 262144 | tf_op jit(solution)/shard_map/all_to_all | solution.py:139
  21.6 2.8 %copy.65 = bf16[1,64,4096]{1,0,2:T(2,128)(2,1)S(1)} copy(bf16[1,64,4096]{2,1,0:T(8,128)(2,1)S(1)} %copy-done) | data formatting | bytes 1048576 | tf_op args[0]
  24.4 22.5 %reduce.6 = bf16[4096,64]{1,0:T(8,128)(2,1)S(1)} reduce(bf16[4096,1,64]{2,1,0:T(2,128)(2,1)S(1)} %bitcast.152, bf16[]{:T(256)} %broadcast.215), dimensions={1}, to_apply=%bitcast.130.reduce_sub_computation | reduce | bytes 1048578
  46.9 1.5 %reshape.158 = bf16[8,2,16384]{2,1,0:T(2,128)(2,1)} reshape(bf16[4096,64]{1,0:T(8,128)(2,1)S(1)} %reduce.6) | data formatting | bytes 1048576
  48.5 5.9 %all-to-all-start.2 = ((bf16[8,2,16384]{2,1,0:T(2,128)(2,1)}), bf16[8,2,16384]{2,1,0:T(2,128)(2,1)}, u32[]{:S(2)}, u32[]{:S(2)}) async-start(bf16[8,2,16384]{2,1,0:T(2,128)(2,1)} %reshape.158), calls=%async_computation.2 | async-start | bytes 1048576 | tf_op jit(solution)/shard_map/all_to_all | solution.py:135
  55.9 6.7 %all_gather.6 = bf16[2048,128]{1,0:T(8,128)(2,1)S(1)} all-gather(bf16[512,128]{1,0:T(8,128)(2,1)S(1)} %bitcast.169), channel_id=1, replica_groups=mesh['ulysses'=8,'blk'=4] {'blk'}, dimensions={0}, use_global_device_ids=true | all-gather | bytes 655360 | tf_op jit(solution)/shard_map/all_gather | solution.py:151
  62.6 7.3 %all_gather.7 = bf16[2048,128]{1,0:T(8,128)(2,1)S(1)} all-gather(bf16[512,128]{1,0:T(8,128)(2,1)S(1)} %bitcast.170), channel_id=1, replica_groups=mesh['ulysses'=8,'blk'=4] {'blk'}, dimensions={0}, use_global_device_ids=true | all-gather | bytes 655360 | tf_op jit(solution)/shard_map/all_gather | solution.py:152
  69.9 4.1 %reshape.159 = bf16[4096,1,64]{2,1,0:T(2,128)(2,1)S(1)} reshape(bf16[8,2,16384]{2,1,0:T(2,128)(2,1)} %all-to-all-done.2) | data formatting | bytes 1048576
  74.0 3.6 %copy.66 = bf16[1,64,4096]{2,1,0:T(8,128)(2,1)} copy(bf16[1,64,4096]{1,0,2:T(2,128)(2,1)S(1)} %bitcast.151) | data formatting | bytes 1048576 | tf_op jit(solution)/shard_map/all_to_all | solution.py:135
  77.6 1.2 copy.81
  79.4 31.0 %while.23 = (s32[]{:T(128)}, f32[1,4,256]{2,1,0:T(4,128)S(1)}, f32[1,4,256]{2,1,0:T(4,128)S(1)}, f32[1,4,256,128]{3,2,1,0:T(8,128)S(1)}, f32[1,4,256]{2,1,0:T(4,...) while((s32[]{:T(128)}, f32[1,4,256]{2,1,0:T(4,128)S(1)}, ...), condition=%wide.region_13.14_spmd, body=%wide.region_1.13_spmd.sunk | while | flops 552381440 | bytes 17462768 | solution.py:103
  79.4 0.6 dynamic_slice.28
  80.8 1.1 fusion.59
  82.5 1.9 %conditional.5 = ((f32[1,4,256]{2,1,0:T(4,128)S(1)}, f32[1,4,256]{2,1,0:T(4,128)S(1)}, f32[1,4,256,128]{3,2,1,0:T(8,128)S(1)})) conditional(s32[]{:T(128)} %convert_element_type.47, (f32[1,4,256]{2,1,0:T(4,128)S(1)}, f32[1,4,256]{2,1,0:T(4,128)S(1)}, f32[1,4,256,128]{3,2,1,0:T(8,128)S(1)}) %tuple.82, (pred[256,512]{0,1:T(8,128)(4,1)S(1)}, ...), branch_computations={%region_9.9_spmd, %region_10.12_spmd} | conditional | flops 275516416 | bytes 8323104 | solution.py:90
  82.5 0.5 fusion.20
  83.0 0.5 fusion.22
  83.6 0.9 fusion.23
  85.2 2.0 %conditional.4 = ((f32[1,4,256]{2,1,0:T(4,128)S(1)}, f32[1,4,256]{2,1,0:T(4,128)S(1)}, f32[1,4,256,128]{3,2,1,0:T(8,128)S(1)})) conditional(s32[]{:T(128)} %convert_element_type.46, (f32[1,4,256]{2,1,0:T(4,128)S(1)}, f32[1,4,256]{2,1,0:T(4,128)S(1)}, f32[1,4,256,128]{3,2,1,0:T(8,128)S(1)}) %tuple.80, (pred[256,512]{0,1:T(8,128)(4,1)S(1)}, ...), branch_computations={%region_4.4_spmd, %region_5.7_spmd} | conditional | flops 275516416 | bytes 8323104 | solution.py:90
  85.2 0.5 fusion
  85.7 0.5 fusion.2
  86.2 0.9 fusion.3
  87.1 0.6 dynamic_slice.28
  88.5 1.1 fusion.59
  90.3 2.0 %conditional.5 = ((f32[1,4,256]{2,1,0:T(4,128)S(1)}, f32[1,4,256]{2,1,0:T(4,128)S(1)}, f32[1,4,256,128]{3,2,1,0:T(8,128)S(1)})) conditional(s32[]{:T(128)} %convert_element_type.47, (f32[1,4,256]{2,1,0:T(4,128)S(1)}, f32[1,4,256]{2,1,0:T(4,128)S(1)}, f32[1,4,256,128]{3,2,1,0:T(8,128)S(1)}) %tuple.82, (pred[256,512]{0,1:T(8,128)(4,1)S(1)}, ...), branch_computations={%region_9.9_spmd, %region_10.12_spmd} | conditional | flops 275516416 | bytes 8323104 | solution.py:90
  90.3 0.5 fusion.20
  90.8 0.5 fusion.22
  91.3 0.9 fusion.23
  92.9 2.0 %conditional.4 = ((f32[1,4,256]{2,1,0:T(4,128)S(1)}, f32[1,4,256]{2,1,0:T(4,128)S(1)}, f32[1,4,256,128]{3,2,1,0:T(8,128)S(1)})) conditional(s32[]{:T(128)} %convert_element_type.46, (f32[1,4,256]{2,1,0:T(4,128)S(1)}, f32[1,4,256]{2,1,0:T(4,128)S(1)}, f32[1,4,256,128]{3,2,1,0:T(8,128)S(1)}) %tuple.80, (pred[256,512]{0,1:T(8,128)(4,1)S(1)}, ...), branch_computations={%region_4.4_spmd, %region_5.7_spmd} | conditional | flops 275516416 | bytes 8323104 | solution.py:90
  92.9 0.5 fusion
  93.4 0.5 fusion.2
  94.0 0.9 fusion.3
  94.9 0.6 dynamic_slice.28
  96.3 1.1 fusion.59
  98.0 1.9 %conditional.5 = ((f32[1,4,256]{2,1,0:T(4,128)S(1)}, f32[1,4,256]{2,1,0:T(4,128)S(1)}, f32[1,4,256,128]{3,2,1,0:T(8,128)S(1)})) conditional(s32[]{:T(128)} %convert_element_type.47, (f32[1,4,256]{2,1,0:T(4,128)S(1)}, f32[1,4,256]{2,1,0:T(4,128)S(1)}, f32[1,4,256,128]{3,2,1,0:T(8,128)S(1)}) %tuple.82, (pred[256,512]{0,1:T(8,128)(4,1)S(1)}, ...), branch_computations={%region_9.9_spmd, %region_10.12_spmd} | conditional | flops 275516416 | bytes 8323104 | solution.py:90
  98.0 0.5 fusion.20
  98.5 0.5 fusion.22
  99.1 0.9 fusion.23
  100.7 2.0 %conditional.4 = ((f32[1,4,256]{2,1,0:T(4,128)S(1)}, f32[1,4,256]{2,1,0:T(4,128)S(1)}, f32[1,4,256,128]{3,2,1,0:T(8,128)S(1)})) conditional(s32[]{:T(128)} %convert_element_type.46, (f32[1,4,256]{2,1,0:T(4,128)S(1)}, f32[1,4,256]{2,1,0:T(4,128)S(1)}, f32[1,4,256,128]{3,2,1,0:T(8,128)S(1)}) %tuple.80, (pred[256,512]{0,1:T(8,128)(4,1)S(1)}, ...), branch_computations={%region_4.4_spmd, %region_5.7_spmd} | conditional | flops 275516416 | bytes 8323104 | solution.py:90
  100.7 0.5 fusion
  101.2 0.5 fusion.2
  101.7 0.9 fusion.3
  102.7 0.6 dynamic_slice.28
  104.0 1.1 fusion.59
  105.8 2.0 %conditional.5 = ((f32[1,4,256]{2,1,0:T(4,128)S(1)}, f32[1,4,256]{2,1,0:T(4,128)S(1)}, f32[1,4,256,128]{3,2,1,0:T(8,128)S(1)})) conditional(s32[]{:T(128)} %convert_element_type.47, (f32[1,4,256]{2,1,0:T(4,128)S(1)}, f32[1,4,256]{2,1,0:T(4,128)S(1)}, f32[1,4,256,128]{3,2,1,0:T(8,128)S(1)}) %tuple.82, (pred[256,512]{0,1:T(8,128)(4,1)S(1)}, ...), branch_computations={%region_9.9_spmd, %region_10.12_spmd} | conditional | flops 275516416 | bytes 8323104 | solution.py:90
  105.8 0.5 fusion.20
  106.3 0.5 fusion.22
  106.9 0.9 fusion.23
  108.4 2.0 %conditional.4 = ((f32[1,4,256]{2,1,0:T(4,128)S(1)}, f32[1,4,256]{2,1,0:T(4,128)S(1)}, f32[1,4,256,128]{3,2,1,0:T(8,128)S(1)})) conditional(s32[]{:T(128)} %convert_element_type.46, (f32[1,4,256]{2,1,0:T(4,128)S(1)}, f32[1,4,256]{2,1,0:T(4,128)S(1)}, f32[1,4,256,128]{3,2,1,0:T(8,128)S(1)}) %tuple.80, (pred[256,512]{0,1:T(8,128)(4,1)S(1)}, ...), branch_computations={%region_4.4_spmd, %region_5.7_spmd} | conditional | flops 275516416 | bytes 8323104 | solution.py:90
  108.4 0.5 fusion
  109.0 0.5 fusion.2
  109.5 0.9 fusion.3
  111.0 0.9 copy.73
  111.9 3.9 %reduce.7 = bf16[512,512]{1,0:T(8,128)(2,1)S(1)} reduce(bf16[512,1,512]{2,1,0:T(2,128)(2,1)S(1)} %bitcast.154, bf16[]{:T(256)} %broadcast.215), dimensions={1}, to_apply=%bitcast.132.reduce_sub_computation | reduce | bytes 1048578
  116.1 20.8 %all_to_all.63 = bf16[8,2,16384]{2,1,0:T(2,128)(2,1)S(1)} all-to-all(bf16[8,2,16384]{2,1,0:T(2,128)(2,1)S(1)} %reshape.160), channel_id=1, replica_groups=mesh['ulysses'=8,'blk'=4] {'ulysses'}, dimensions={0} | all-to-all | bytes 1048576 | tf_op jit(solution)/shard_map/all_to_all | solution.py:156
  136.9 0.5 reshape.161
  137.6 0.8 copy.78
  (84 shorter events, 4.2 us)
Async XLA Ops:
  0.0 10.9 %copy-start.1 = (bf16[1,64,1024]{2,1,0:T(8,128)(2,1)S(1)}, bf16[1,64,1024]{2,1,0:T(8,128)(2,1)}, u32[]{:S(2)}) copy-start(bf16[1,64,1024]{2,1,0:T(8,128)(2,1)} %param.12) | copy-start | bytes 393220
  0.0 21.6 %copy-start = (bf16[1,64,4096]{2,1,0:T(8,128)(2,1)S(1)}, bf16[1,64,4096]{2,1,0:T(8,128)(2,1)}, u32[]{:S(2)}) copy-start(bf16[1,64,4096]{2,1,0:T(8,128)(2,1)} %param.10) | copy-start | bytes 1572868
  5.1 13.1 %all-to-all-start = ((bf16[8,2,4096]{2,1,0:T(2,128)(2,1)}), bf16[8,2,4096]{2,1,0:T(2,128)(2,1)S(1)}, u32[]{:S(2)}, u32[]{:S(2)}) async-start(bf16[8,2,4096]{2,1,0:T(2,128)(2,1)} %reshape.154), calls=%async_computation | async-start | bytes 262144 | tf_op jit(solution)/shard_map/all_to_all | solution.py:136
  18.2 30.3 %all-to-all-start.1 = ((bf16[8,2,4096]{2,1,0:T(2,128)(2,1)}), bf16[8,2,4096]{2,1,0:T(2,128)(2,1)S(1)}, u32[]{:S(2)}, u32[]{:S(2)}) async-start(bf16[8,2,4096]{2,1,0:T(2,128)(2,1)} %reshape.156), calls=%async_computation.1 | async-start | bytes 262144 | tf_op jit(solution)/shard_map/all_to_all | solution.py:139
  24.4 24.0 %copy-start.2 = (s32[16]{0:T(128)S(1)}, s32[16]{0:T(128)}, u32[]{:S(2)}) copy-start(s32[16]{0:T(128)} %param.13) | copy-start | bytes 196
  48.5 21.3 %all-to-all-start.2 = ((bf16[8,2,16384]{2,1,0:T(2,128)(2,1)}), bf16[8,2,16384]{2,1,0:T(2,128)(2,1)}, u32[]{:S(2)}, u32[]{:S(2)}) async-start(bf16[8,2,16384]{2,1,0:T(2,128)(2,1)} %reshape.158), calls=%async_computation.2 | async-start | bytes 1048576 | tf_op jit(solution)/shard_map/all_to_all | solution.py:135
where the time goes:
time: 139 us; the launch traced here: 138 us
  other arithmetic  40.5 us (29%)
  blocking collectives  34.7 us (25%)
  local copies, waits for them, and re-layouts  24.7 us (18%)
  starting transfers between devices  15.1 us (11%)
  matrix products  10.8 us (8%)
  loops' own time  8.49 us (6%)
  waiting for transfers between devices  3.74 us (3%)
    unnamed x4, other arithmetic  31 us
    all_to_all x1, blocking collectives, local(): lax.all_to_all(finish(running)[None], 'ulysses', split_axis=1, concat_axi...  20.8 us
    unnamed x22, local copies, waits for them, and re-layouts  15.4 us
    another operation x1, loops' own time, fold_step(): lax.scan(one_block, running, (key_blocks, value_blocks, jnp.arange(block_...  8.16 us
    all_gather x1, blocking collectives, local(): lax.all_gather(value_local, 'blk', axis=0, tiled=True)  7.26 us
    dot_general x8, matrix products, update(): jnp.einsum('kgqs,skd->kgqd', weights.astype(jnp.bfloat16), value_block, p...  6.93 us
    all_gather x1, blocking collectives, local(): lax.all_gather(key_local, 'blk', axis=0, tiled=True)  6.68 us
    all_to_all x1, starting transfers between devices, local(): lax.all_to_all(queries, 'ulysses', split_axis=2, concat_axis=1, tiled=True)  5.9 us
  transfers between devices with their start and end apart: 3, of which 1 were waited for; matrix products, arithmetic and copies ran while one was open for 23% of the time, Pallas kernels for 0%

commit v1 on v0

--- a/solution.py
+++ b/solution.py
@@ -7,6 +7,18 @@
 HEAD_DIM = 128
 TILE = 128
 masked_score = -1e30
+
+
+def cut_along(value, dim, size):
+    dims = value.shape
+    pieces = value.reshape(*dims[:dim], size, dims[dim] // size, *dims[dim + 1 :])
+    return jnp.moveaxis(pieces, dim, 0)
+
+
+def in_order(blocks, dim):
+    blocks = jnp.moveaxis(blocks, 0, dim)
+    shape = blocks.shape
+    return blocks.reshape(*shape[:dim], shape[dim] * shape[dim + 1], *shape[dim + 2 :])
 
 
 def segment_of(positions, tile_segment):
@@ -153,9 +165,15 @@
         ),
         jnp.int32(0),
     )
-    attended = lax.all_to_all(
-        finish(running)[None], "ulysses", split_axis=1, concat_axis=2, tiled=True
-    )
+    array = finish(running)[None]
+    size, place = (lax.axis_size("ulysses"), lax.axis_index("ulysses"))
+    pieces = cut_along(array, 1, size)
+    done = [pieces[place]]
+    for step in range(1, size):
+        sent = pieces[place ^ step]
+        done.append(lax.ppermute(sent, "ulysses", [(i, i ^ step) for i in range(size)]))
+    pieces = jnp.stack(done)[place ^ jnp.arange(size)]
+    attended = in_order(pieces, 2)
     return attended
 
 

time: 139 us -> 133 us (0.957); the launches traced: 138 us -> 131 us
  blocking collectives: 34.7 us -> 13.9 us
  starting transfers between devices: 15.1 us -> 26.5 us
  waiting for transfers between devices: 3.74 us -> 10.7 us
  other arithmetic: 40.5 us -> 36.7 us
    all_to_all x1 -> x0, blocking collectives: 20.8 us -> none  [local(): lax.all_to_all(finish(running)[None], 'ulysses', split_axis=1, concat_axi...]
    ppermute x0 -> x7, starting transfers between devices: none -> 11.3 us  [local(): lax.ppermute(sent, 'ulysses', [(i, i ^ step) for i in range(size)])]
    ppermute x0 -> x7, waiting for transfers between devices: none -> 6.91 us  [local(): lax.ppermute(sent, 'ulysses', [(i, i ^ step) for i in range(size)])]
    unnamed x4 -> x3, other arithmetic: 31 us -> 26.9 us
    unnamed x22 -> x25, local copies, waits for them, and re-layouts: 15.4 us -> 14.4 us
  transfers between devices with their start and end apart: 3 -> 10, of which waited for: 1 -> 3; matrix products, arithmetic and copies ran while one was open for 23% -> 24% of each run, Pallas kernels for 0% -> 0%
where the time goes in v1:
time: 133 us; the launch traced here: 131 us
  other arithmetic  36.7 us (28%)
  starting transfers between devices  26.5 us (20%)
  local copies, waits for them, and re-layouts  23.7 us (18%)
  blocking collectives  13.9 us (10%)
  matrix products  10.8 us (8%)
  waiting for transfers between devices  10.7 us (8%)
  loops' own time  8.25 us (6%)
    unnamed x3, other arithmetic  26.9 us
    unnamed x25, local copies, waits for them, and re-layouts  14.4 us
    ppermute x7, starting transfers between devices, local(): lax.ppermute(sent, 'ulysses', [(i, i ^ step) for i in range(size)])  11.3 us
    another operation x1, loops' own time, fold_step(): lax.scan(one_block, running, (key_blocks, value_blocks, jnp.arange(block_...  7.92 us
    all_gather x1, blocking collectives, local(): lax.all_gather(value_local, 'blk', axis=0, tiled=True)  7.26 us
    dot_general x8, matrix products, update(): jnp.einsum('kgqs,skd->kgqd', weights.astype(jnp.bfloat16), value_block, p...  6.93 us
    ppermute x7, waiting for transfers between devices, local(): lax.ppermute(sent, 'ulysses', [(i, i ^ step) for i in range(size)])  6.91 us
    all_gather x1, blocking collectives, local(): lax.all_gather(key_local, 'blk', axis=0, tiled=True)  6.68 us
  transfers between devices with their start and end apart: 10, of which 3 were waited for; matrix products, arithmetic and copies ran while one was open for 24% of the time, Pallas kernels for 0%

profile of v1, /device:TPU:4, one launch (start us, length us, event | category | flops | bytes accessed | tf_op | source)
XLA Modules:
  0.0 130.9 jit_solution(507074064834397227)
XLA Ops:
  0.0 1.3 copy.51
  1.3 0.5 broadcast.254
  1.8 2.3 %reduce.4 = bf16[1024,64]{1,0:T(8,128)(2,1)S(1)} reduce(bf16[1024,1,64]{2,1,0:T(2,128)(2,1)S(1)} %bitcast.188, bf16[]{:T(256)} %broadcast.254), dimensions={1}, to_apply=%bitcast.158.reduce_sub_computation | reduce | bytes 262146
  4.1 0.9 reshape.184
  5.0 5.8 %all-to-all-start = ((bf16[8,2,4096]{2,1,0:T(2,128)(2,1)}), bf16[8,2,4096]{2,1,0:T(2,128)(2,1)S(1)}, u32[]{:S(2)}, u32[]{:S(2)}) async-start(bf16[8,2,4096]{2,1,0:T(2,128)(2,1)} %reshape.184), calls=%async_computation | async-start | bytes 262144 | tf_op jit(solution)/shard_map/all_to_all | solution.py:148
  11.2 2.3 %reduce.5 = bf16[1024,64]{1,0:T(8,128)(2,1)S(1)} reduce(bf16[1024,1,64]{2,1,0:T(2,128)(2,1)S(1)} %bitcast.189, bf16[]{:T(256)} %broadcast.254), dimensions={1}, to_apply=%bitcast.160.reduce_sub_computation | reduce | bytes 262146
  13.5 0.9 reshape.186
  14.4 3.8 %all-to-all-done = bf16[8,2,4096]{2,1,0:T(2,128)(2,1)S(1)} async-done(((bf16[8,2,4096]{2,1,0:T(2,128)(2,1)}), bf16[8,2,4096]{2,1,0:T(2,128)(2,1)S(1)}, u32[]{:S(2)}, u32[]{:S(2)}) %all-to-all-start) | async-done | bytes 131104 | tf_op jit(solution)/shard_map/all_to_all | solution.py:148
  18.1 3.4 %all-to-all-start.1 = ((bf16[8,2,4096]{2,1,0:T(2,128)(2,1)}), bf16[8,2,4096]{2,1,0:T(2,128)(2,1)S(1)}, u32[]{:S(2)}, u32[]{:S(2)}) async-start(bf16[8,2,4096]{2,1,0:T(2,128)(2,1)} %reshape.186), calls=%async_computation.1 | async-start | bytes 262144 | tf_op jit(solution)/shard_map/all_to_all | solution.py:151
  21.6 2.8 %copy.57 = bf16[1,64,4096]{1,0,2:T(2,128)(2,1)S(1)} copy(bf16[1,64,4096]{2,1,0:T(8,128)(2,1)S(1)} %copy-done) | data formatting | bytes 1048576 | tf_op args[0]
  24.4 22.4 %reduce.6 = bf16[4096,64]{1,0:T(8,128)(2,1)S(1)} reduce(bf16[4096,1,64]{2,1,0:T(2,128)(2,1)S(1)} %bitcast.182, bf16[]{:T(256)} %broadcast.254), dimensions={1}, to_apply=%bitcast.162.reduce_sub_computation | reduce | bytes 1048578
  46.8 1.5 %reshape.188 = bf16[8,2,16384]{2,1,0:T(2,128)(2,1)} reshape(bf16[4096,64]{1,0:T(8,128)(2,1)S(1)} %reduce.6) | data formatting | bytes 1048576
  48.3 5.9 %all-to-all-start.2 = ((bf16[8,2,16384]{2,1,0:T(2,128)(2,1)}), bf16[8,2,16384]{2,1,0:T(2,128)(2,1)}, u32[]{:S(2)}, u32[]{:S(2)}) async-start(bf16[8,2,16384]{2,1,0:T(2,128)(2,1)} %reshape.188), calls=%async_computation.2 | async-start | bytes 1048576 | tf_op jit(solution)/shard_map/all_to_all | solution.py:147
  55.7 6.7 %all_gather.6 = bf16[2048,128]{1,0:T(8,128)(2,1)S(1)} all-gather(bf16[512,128]{1,0:T(8,128)(2,1)S(1)} %bitcast.197), channel_id=1, replica_groups=mesh['ulysses'=8,'blk'=4] {'blk'}, dimensions={0}, use_global_device_ids=true | all-gather | bytes 655360 | tf_op jit(solution)/shard_map/all_gather | solution.py:163
  62.4 7.3 %all_gather.7 = bf16[2048,128]{1,0:T(8,128)(2,1)S(1)} all-gather(bf16[512,128]{1,0:T(8,128)(2,1)S(1)} %bitcast.198), channel_id=1, replica_groups=mesh['ulysses'=8,'blk'=4] {'blk'}, dimensions={0}, use_global_device_ids=true | all-gather | bytes 655360 | tf_op jit(solution)/shard_map/all_gather | solution.py:164
  69.7 4.1 %reshape.189 = bf16[4096,1,64]{2,1,0:T(2,128)(2,1)S(1)} reshape(bf16[8,2,16384]{2,1,0:T(2,128)(2,1)} %all-to-all-done.2) | data formatting | bytes 1048576
  73.8 3.6 %copy.58 = bf16[1,64,4096]{2,1,0:T(8,128)(2,1)} copy(bf16[1,64,4096]{1,0,2:T(2,128)(2,1)S(1)} %bitcast.181) | data formatting | bytes 1048576 | tf_op jit(solution)/shard_map/all_to_all | solution.py:147
  77.4 1.2 copy.70
  79.2 30.7 %while.23 = (s32[]{:T(128)}, f32[1,4,256]{2,1,0:T(4,128)S(1)}, f32[1,4,256]{2,1,0:T(4,128)S(1)}, f32[1,4,256,128]{3,2,1,0:T(8,128)S(1)}, f32[1,4,256]{2,1,0:T(4,...) while((s32[]{:T(128)}, f32[1,4,256]{2,1,0:T(4,128)S(1)}, ...), condition=%wide.region_13.14_spmd, body=%wide.region_1.13_spmd.sunk | while | flops 552381440 | bytes 17462768 | solution.py:115
  79.2 0.6 dynamic_slice.68
  80.6 1.1 fusion.60
  82.3 1.9 %conditional.5 = ((f32[1,4,256]{2,1,0:T(4,128)S(1)}, f32[1,4,256]{2,1,0:T(4,128)S(1)}, f32[1,4,256,128]{3,2,1,0:T(8,128)S(1)})) conditional(s32[]{:T(128)} %convert_element_type.47, (f32[1,4,256]{2,1,0:T(4,128)S(1)}, f32[1,4,256]{2,1,0:T(4,128)S(1)}, f32[1,4,256,128]{3,2,1,0:T(8,128)S(1)}) %tuple.89, (pred[256,512]{0,1:T(8,128)(4,1)S(1)}, ...), branch_computations={%region_9.9_spmd, %region_10.12_spmd} | conditional | flops 275516416 | bytes 8323104 | solution.py:102
  82.8 0.5 fusion.22
  83.4 0.9 fusion.23
  84.9 2.0 %conditional.4 = ((f32[1,4,256]{2,1,0:T(4,128)S(1)}, f32[1,4,256]{2,1,0:T(4,128)S(1)}, f32[1,4,256,128]{3,2,1,0:T(8,128)S(1)})) conditional(s32[]{:T(128)} %convert_element_type.46, (f32[1,4,256]{2,1,0:T(4,128)S(1)}, f32[1,4,256]{2,1,0:T(4,128)S(1)}, f32[1,4,256,128]{3,2,1,0:T(8,128)S(1)}) %tuple.87, (pred[256,512]{0,1:T(8,128)(4,1)S(1)}, ...), branch_computations={%region_4.4_spmd, %region_5.7_spmd} | conditional | flops 275516416 | bytes 8323104 | solution.py:102
  84.9 0.5 fusion
  85.4 0.5 fusion.2
  86.0 0.9 fusion.3
  86.9 0.6 dynamic_slice.68
  88.3 1.1 fusion.60
  90.0 2.0 %conditional.5 = ((f32[1,4,256]{2,1,0:T(4,128)S(1)}, f32[1,4,256]{2,1,0:T(4,128)S(1)}, f32[1,4,256,128]{3,2,1,0:T(8,128)S(1)})) conditional(s32[]{:T(128)} %convert_element_type.47, (f32[1,4,256]{2,1,0:T(4,128)S(1)}, f32[1,4,256]{2,1,0:T(4,128)S(1)}, f32[1,4,256,128]{3,2,1,0:T(8,128)S(1)}) %tuple.89, (pred[256,512]{0,1:T(8,128)(4,1)S(1)}, ...), branch_computations={%region_9.9_spmd, %region_10.12_spmd} | conditional | flops 275516416 | bytes 8323104 | solution.py:102
  90.5 0.5 fusion.22
  91.1 0.9 fusion.23
  92.6 2.0 %conditional.4 = ((f32[1,4,256]{2,1,0:T(4,128)S(1)}, f32[1,4,256]{2,1,0:T(4,128)S(1)}, f32[1,4,256,128]{3,2,1,0:T(8,128)S(1)})) conditional(s32[]{:T(128)} %convert_element_type.46, (f32[1,4,256]{2,1,0:T(4,128)S(1)}, f32[1,4,256]{2,1,0:T(4,128)S(1)}, f32[1,4,256,128]{3,2,1,0:T(8,128)S(1)}) %tuple.87, (pred[256,512]{0,1:T(8,128)(4,1)S(1)}, ...), branch_computations={%region_4.4_spmd, %region_5.7_spmd} | conditional | flops 275516416 | bytes 8323104 | solution.py:102
  92.6 0.5 fusion
  93.1 0.5 fusion.2
  93.7 0.9 fusion.3
  94.6 0.6 dynamic_slice.68
  95.9 1.1 fusion.60
  97.7 2.0 %conditional.5 = ((f32[1,4,256]{2,1,0:T(4,128)S(1)}, f32[1,4,256]{2,1,0:T(4,128)S(1)}, f32[1,4,256,128]{3,2,1,0:T(8,128)S(1)})) conditional(s32[]{:T(128)} %convert_element_type.47, (f32[1,4,256]{2,1,0:T(4,128)S(1)}, f32[1,4,256]{2,1,0:T(4,128)S(1)}, f32[1,4,256,128]{3,2,1,0:T(8,128)S(1)}) %tuple.89, (pred[256,512]{0,1:T(8,128)(4,1)S(1)}, ...), branch_computations={%region_9.9_spmd, %region_10.12_spmd} | conditional | flops 275516416 | bytes 8323104 | solution.py:102
  98.2 0.5 fusion.22
  98.8 0.9 fusion.23
  100.3 2.0 %conditional.4 = ((f32[1,4,256]{2,1,0:T(4,128)S(1)}, f32[1,4,256]{2,1,0:T(4,128)S(1)}, f32[1,4,256,128]{3,2,1,0:T(8,128)S(1)})) conditional(s32[]{:T(128)} %convert_element_type.46, (f32[1,4,256]{2,1,0:T(4,128)S(1)}, f32[1,4,256]{2,1,0:T(4,128)S(1)}, f32[1,4,256,128]{3,2,1,0:T(8,128)S(1)}) %tuple.87, (pred[256,512]{0,1:T(8,128)(4,1)S(1)}, ...), branch_computations={%region_4.4_spmd, %region_5.7_spmd} | conditional | flops 275516416 | bytes 8323104 | solution.py:102
  100.3 0.5 fusion
  100.8 0.5 fusion.2
  101.4 0.9 fusion.3
  102.3 0.6 dynamic_slice.68
  103.6 1.1 fusion.60
  105.4 2.0 %conditional.5 = ((f32[1,4,256]{2,1,0:T(4,128)S(1)}, f32[1,4,256]{2,1,0:T(4,128)S(1)}, f32[1,4,256,128]{3,2,1,0:T(8,128)S(1)})) conditional(s32[]{:T(128)} %convert_element_type.47, (f32[1,4,256]{2,1,0:T(4,128)S(1)}, f32[1,4,256]{2,1,0:T(4,128)S(1)}, f32[1,4,256,128]{3,2,1,0:T(8,128)S(1)}) %tuple.89, (pred[256,512]{0,1:T(8,128)(4,1)S(1)}, ...), branch_computations={%region_9.9_spmd, %region_10.12_spmd} | conditional | flops 275516416 | bytes 8323104 | solution.py:102
  105.9 0.5 fusion.22
  106.4 0.9 fusion.23
  108.0 2.0 %conditional.4 = ((f32[1,4,256]{2,1,0:T(4,128)S(1)}, f32[1,4,256]{2,1,0:T(4,128)S(1)}, f32[1,4,256,128]{3,2,1,0:T(8,128)S(1)})) conditional(s32[]{:T(128)} %convert_element_type.46, (f32[1,4,256]{2,1,0:T(4,128)S(1)}, f32[1,4,256]{2,1,0:T(4,128)S(1)}, f32[1,4,256,128]{3,2,1,0:T(8,128)S(1)}) %tuple.87, (pred[256,512]{0,1:T(8,128)(4,1)S(1)}, ...), branch_computations={%region_4.4_spmd, %region_5.7_spmd} | conditional | flops 275516416 | bytes 8323104 | solution.py:102
  108.0 0.5 fusion
  108.5 0.5 fusion.2
  109.0 0.9 fusion.3
  111.1 2.1 %collective-permute-start = (bf16[1,64,512]{2,1,0:T(8,128)(2,1)S(1)}, bf16[1,64,512]{2,1,0:T(8,128)(2,1)S(1)}, u32[]{:S(2)}, u32[]{:S(2)}) collective-permute-start(bf16[1,64,512]{2,1,0:T(8,128)(2,1)S(1)} %get-tuple-element.476), channel_id=1, source_target_pairs={{0,4},{4,0},{8,12},{12,8},{16,20},{20,16},{24,28},{28,24},{1,5},{5... | collective-permute-start | bytes 196616 | tf_op jit(solution)/shard_map/ppermute | solution.py:174
  113.2 1.5 %collective-permute-start.1 = (bf16[1,64,512]{2,1,0:T(8,128)(2,1)S(1)}, bf16[1,64,512]{2,1,0:T(8,128)(2,1)S(1)}, u32[]{:S(2)}, u32[]{:S(2)}) collective-permute-start(bf16[1,64,512]{2,1,0:T(8,128)(2,1)S(1)} %get-tuple-element.475), channel_id=1, source_target_pairs={{0,8},{4,12},{8,0},{12,4},{16,24},{20,28},{24,16},{28,20},{1,9},{5... | collective-permute-start | bytes 196616 | tf_op jit(solution)/shard_map/ppermute | solution.py:174
  114.7 2.8 %collective-permute-start.3 = (bf16[1,64,512]{2,1,0:T(8,128)(2,1)S(1)}, bf16[1,64,512]{2,1,0:T(8,128)(2,1)S(1)}, u32[]{:S(2)}, u32[]{:S(2)}) collective-permute-start(bf16[1,64,512]{2,1,0:T(8,128)(2,1)S(1)} %get-tuple-element.473), channel_id=1, source_target_pairs={{0,16},{4,20},{8,24},{12,28},{16,0},{20,4},{24,8},{28,12},{1,17},{... | collective-permute-start | bytes 196616 | tf_op jit(solution)/shard_map/ppermute | solution.py:174
  117.6 1.5 %collective-permute-start.4 = (bf16[1,64,512]{2,1,0:T(8,128)(2,1)S(1)}, bf16[1,64,512]{2,1,0:T(8,128)(2,1)S(1)}, u32[]{:S(2)}, u32[]{:S(2)}) collective-permute-start(bf16[1,64,512]{2,1,0:T(8,128)(2,1)S(1)} %get-tuple-element.472), channel_id=1, source_target_pairs={{0,20},{4,16},{8,28},{12,24},{16,4},{20,0},{24,12},{28,8},{1,21},{... | collective-permute-start | bytes 196616 | tf_op jit(solution)/shard_map/ppermute | solution.py:174
  119.0 3.3 %collective-permute-start.5 = (bf16[1,64,512]{2,1,0:T(8,128)(2,1)S(1)}, bf16[1,64,512]{2,1,0:T(8,128)(2,1)S(1)}, u32[]{:S(2)}, u32[]{:S(2)}) collective-permute-start(bf16[1,64,512]{2,1,0:T(8,128)(2,1)S(1)} %get-tuple-element.471), channel_id=1, source_target_pairs={{0,24},{4,28},{8,16},{12,20},{16,8},{20,12},{24,0},{28,4},{1,25},{... | collective-permute-start | bytes 196616 | tf_op jit(solution)/shard_map/ppermute | solution.py:174
  122.5 5.5 %collective-permute-done.4 = bf16[1,64,512]{2,1,0:T(8,128)(2,1)S(1)} collective-permute-done((bf16[1,64,512]{2,1,0:T(8,128)(2,1)S(1)}, bf16[1,64,512]{2,1,0:T(8,128)(2,1)S(1)}, u32[]{:S(2)}, u32[]{:S(2)}) %collective-permute-start.4) | collective-permute-done | bytes 65568 | tf_op jit(solution)/shard_map/ppermute | solution.py:174
  128.0 1.4 %collective-permute-done.6 = bf16[1,64,512]{2,1,0:T(8,128)(2,1)S(1)} collective-permute-done((bf16[1,64,512]{2,1,0:T(8,128)(2,1)S(1)}, bf16[1,64,512]{2,1,0:T(8,128)(2,1)S(1)}, u32[]{:S(2)}, u32[]{:S(2)}) %collective-permute-start.6) | collective-permute-done | bytes 65568 | tf_op jit(solution)/shard_map/ppermute | solution.py:174
  129.4 0.6 gather_fusion
  130.0 0.8 copy.67
  (103 shorter events, 6.5 us)
Async XLA Ops:
  0.0 10.8 %copy-start.1 = (bf16[1,64,1024]{2,1,0:T(8,128)(2,1)S(1)}, bf16[1,64,1024]{2,1,0:T(8,128)(2,1)}, u32[]{:S(2)}) copy-start(bf16[1,64,1024]{2,1,0:T(8,128)(2,1)} %param.12) | copy-start | bytes 393220
  0.0 21.5 %copy-start.2 = (s32[16]{0:T(128)S(1)}, s32[16]{0:T(128)}, u32[]{:S(2)}) copy-start(s32[16]{0:T(128)} %param.13) | copy-start | bytes 196
  0.0 21.6 %copy-start = (bf16[1,64,4096]{2,1,0:T(8,128)(2,1)S(1)}, bf16[1,64,4096]{2,1,0:T(8,128)(2,1)}, u32[]{:S(2)}) copy-start(bf16[1,64,4096]{2,1,0:T(8,128)(2,1)} %param.10) | copy-start | bytes 1572868
  5.0 13.1 %all-to-all-start = ((bf16[8,2,4096]{2,1,0:T(2,128)(2,1)}), bf16[8,2,4096]{2,1,0:T(2,128)(2,1)S(1)}, u32[]{:S(2)}, u32[]{:S(2)}) async-start(bf16[8,2,4096]{2,1,0:T(2,128)(2,1)} %reshape.184), calls=%async_computation | async-start | bytes 262144 | tf_op jit(solution)/shard_map/all_to_all | solution.py:148
  18.1 30.2 %all-to-all-start.1 = ((bf16[8,2,4096]{2,1,0:T(2,128)(2,1)}), bf16[8,2,4096]{2,1,0:T(2,128)(2,1)S(1)}, u32[]{:S(2)}, u32[]{:S(2)}) async-start(bf16[8,2,4096]{2,1,0:T(2,128)(2,1)} %reshape.186), calls=%async_computation.1 | async-start | bytes 262144 | tf_op jit(solution)/shard_map/all_to_all | solution.py:151
  48.3 21.4 %all-to-all-start.2 = ((bf16[8,2,16384]{2,1,0:T(2,128)(2,1)}), bf16[8,2,16384]{2,1,0:T(2,128)(2,1)}, u32[]{:S(2)}, u32[]{:S(2)}) async-start(bf16[8,2,16384]{2,1,0:T(2,128)(2,1)} %reshape.188), calls=%async_computation.2 | async-start | bytes 1048576 | tf_op jit(solution)/shard_map/all_to_all | solution.py:147
  111.1 7.9 %collective-permute-start = (bf16[1,64,512]{2,1,0:T(8,128)(2,1)S(1)}, bf16[1,64,512]{2,1,0:T(8,128)(2,1)S(1)}, u32[]{:S(2)}, u32[]{:S(2)}) collective-permute-start(bf16[1,64,512]{2,1,0:T(8,128)(2,1)S(1)} %get-tuple-element.476), channel_id=1, source_target_pairs={{0,4},{4,0},{8,12},{12,8},{16,20},{20,16},{24,28},{28,24},{1,5},{5... | collective-permute-start | bytes 196616 | tf_op jit(solution)/shard_map/ppermute | solution.py:174
  113.2 9.1 %collective-permute-start.1 = (bf16[1,64,512]{2,1,0:T(8,128)(2,1)S(1)}, bf16[1,64,512]{2,1,0:T(8,128)(2,1)S(1)}, u32[]{:S(2)}, u32[]{:S(2)}) collective-permute-start(bf16[1,64,512]{2,1,0:T(8,128)(2,1)S(1)} %get-tuple-element.475), channel_id=1, source_target_pairs={{0,8},{4,12},{8,0},{12,4},{16,24},{20,28},{24,16},{28,20},{1,9},{5... | collective-permute-start | bytes 196616 | tf_op jit(solution)/shard_map/ppermute | solution.py:174
  114.6 7.8 %collective-permute-start.2 = (bf16[1,64,512]{2,1,0:T(8,128)(2,1)S(1)}, bf16[1,64,512]{2,1,0:T(8,128)(2,1)S(1)}, u32[]{:S(2)}, u32[]{:S(2)}) collective-permute-start(bf16[1,64,512]{2,1,0:T(8,128)(2,1)S(1)} %get-tuple-element.474), channel_id=1, source_target_pairs={{0,12},{4,8},{8,4},{12,0},{16,28},{20,24},{24,20},{28,16},{1,13},{... | collective-permute-start | bytes 196616 | tf_op jit(solution)/shard_map/ppermute | solution.py:174
  114.7 7.8 %collective-permute-start.3 = (bf16[1,64,512]{2,1,0:T(8,128)(2,1)S(1)}, bf16[1,64,512]{2,1,0:T(8,128)(2,1)S(1)}, u32[]{:S(2)}, u32[]{:S(2)}) collective-permute-start(bf16[1,64,512]{2,1,0:T(8,128)(2,1)S(1)} %get-tuple-element.473), channel_id=1, source_target_pairs={{0,16},{4,20},{8,24},{12,28},{16,0},{20,4},{24,8},{28,12},{1,17},{... | collective-permute-start | bytes 196616 | tf_op jit(solution)/shard_map/ppermute | solution.py:174
  117.6 10.4 %collective-permute-start.4 = (bf16[1,64,512]{2,1,0:T(8,128)(2,1)S(1)}, bf16[1,64,512]{2,1,0:T(8,128)(2,1)S(1)}, u32[]{:S(2)}, u32[]{:S(2)}) collective-permute-start(bf16[1,64,512]{2,1,0:T(8,128)(2,1)S(1)} %get-tuple-element.472), channel_id=1, source_target_pairs={{0,20},{4,16},{8,28},{12,24},{16,4},{20,0},{24,12},{28,8},{1,21},{... | collective-permute-start | bytes 196616 | tf_op jit(solution)/shard_map/ppermute | solution.py:174
  119.0 9.0 %collective-permute-start.5 = (bf16[1,64,512]{2,1,0:T(8,128)(2,1)S(1)}, bf16[1,64,512]{2,1,0:T(8,128)(2,1)S(1)}, u32[]{:S(2)}, u32[]{:S(2)}) collective-permute-start(bf16[1,64,512]{2,1,0:T(8,128)(2,1)S(1)} %get-tuple-element.471), channel_id=1, source_target_pairs={{0,24},{4,28},{8,16},{12,20},{16,8},{20,12},{24,0},{28,4},{1,25},{... | collective-permute-start | bytes 196616 | tf_op jit(solution)/shard_map/ppermute | solution.py:174
  122.3 7.1 %collective-permute-start.6 = (bf16[1,64,512]{2,1,0:T(8,128)(2,1)S(1)}, bf16[1,64,512]{2,1,0:T(8,128)(2,1)S(1)}, u32[]{:S(2)}, u32[]{:S(2)}) collective-permute-start(bf16[1,64,512]{2,1,0:T(8,128)(2,1)S(1)} %get-tuple-element.470), channel_id=1, source_target_pairs={{0,28},{4,24},{8,20},{12,16},{16,12},{20,8},{24,4},{28,0},{1,29},{... | collective-permute-start | bytes 196616 | tf_op jit(solution)/shard_map/ppermute | solution.py:174
